TPU v7x, 32 devices: a whole 2x2x4 slice. The times are simulated.
32 devices in a mesh: rows: 8 (over y, x, core), sub: 4 (over z).
Axes of the slice: x: 2, y: 2, z: 4, core: 2. Of those that a mesh axis runs over, the one named last changes fastest.
Arguments:
- u_fem: float32 [120, 524288], P(None, ('rows', 'sub')), may hold values from -600 to 600
- resid_fem: float32 [1, 524288], P(None, ('rows', 'sub')), may hold values from -60 to 60
- slot_map: int32 [32, 32], P(('rows', 'sub')), may hold values from 0 to 31, as said below
- restart: float32 [120, 40], replicated, may hold values from -0.5 to 0.5
- coeff: float32 [3, 120, 120], P(None, None, 'sub'), may hold values from -6 to 6
Outputs:
- new_basis: float32 [40, 524288], P(None, ('rows', 'sub'))
- next_vector: float32 [1, 524288], P(None, ('rows', 'sub'))
- new_coeff: float32 [3, 40, 120], replicated
Inputs may be any that keep to these rules, and one draw needn't show every extreme that they name: Each row of slot_map is a permutation of 0 to 31.
All inputs are finite; a program needn't handle non-finite values.
Results may differ from a plain program's by a relative error of at most 0.00015.
Values sent between devices are 32-bit elements; how exact they have to be, the bound alone decides.
A program may use at most 64 MiB of HBM per device.

v0:
```python
import jax
import jax.numpy as jnp
from jax import lax
from jax.sharding import PartitionSpec as P


def settle(values, source, dev_count):
    width = values.shape[0]
    block_len = values.shape[1] // dev_count
    blocks = values.reshape(width, dev_count, block_len)
    return jnp.take(blocks, source, axis=1).reshape(width, dev_count * block_len)


def local(u_fem, resid_fem, slot_map, restart, coeff):
    highest = lax.Precision.HIGHEST
    dev_count = lax.axis_size(("rows", "sub"))
    nrows_all = u_fem.shape[1] * dev_count
    source = jnp.argsort(slot_map[0])
    basis_rows, resid_row = (u_fem, resid_fem)
    gram_local = jnp.einsum("kn,jn->kj", basis_rows, basis_rows, precision=highest)
    inner_local = jnp.einsum("kn,n->k", basis_rows, resid_row[0], precision=highest)
    gram_sum = lax.psum(gram_local, ("rows", "sub"))
    chol_lower = jnp.linalg.cholesky(gram_sum / nrows_all)
    factor = lax.linalg.triangular_solve(
        chol_lower, restart, left_side=True, lower=True, transpose_a=True
    )
    new_rows = jnp.einsum("kp,kn->pn", factor, basis_rows, precision=highest)
    inner_prod = lax.psum(inner_local, ("rows", "sub"))
    half_solve = lax.linalg.triangular_solve(
        chol_lower, inner_prod[:, None], left_side=True, lower=True
    )
    proj_coef = (
        lax.linalg.triangular_solve(
            chol_lower, half_solve, left_side=True, lower=True, transpose_a=True
        )[:, 0]
        / nrows_all
    )
    remainder = resid_row - jnp.einsum("k,kn->n", proj_coef, basis_rows, precision=highest)[None, :]
    norm_sum = lax.psum(jnp.sum(remainder * remainder), ("rows", "sub"))
    next_row = remainder * lax.rsqrt(norm_sum / nrows_all + 1e-06)
    new_rows, next_row = (
        lax.all_to_all(new_rows, ("rows", "sub"), split_axis=1, concat_axis=1, tiled=True),
        lax.all_to_all(next_row, ("rows", "sub"), split_axis=1, concat_axis=1, tiled=True),
    )
    new_rows = settle(new_rows, source, dev_count)
    next_row = settle(next_row, source, dev_count)
    raised = jnp.dot(chol_lower, restart, precision=highest)
    coeff_all = lax.all_gather(coeff, "sub", axis=2, tiled=True)
    rotated = jnp.einsum("kp,ikm->ipm", raised, coeff_all, precision=highest)
    new_coeff = rotated * lax.rsqrt(jnp.mean(rotated * rotated) + 1e-06)
    return (new_rows, next_row, new_coeff)


def solution(mesh):
    in_specs = (
        P(None, ("rows", "sub")),
        P(None, ("rows", "sub")),
        P(("rows", "sub"), None),
        P(),
        P(None, None, "sub"),
    )
    out_specs = (P(None, ("rows", "sub")), P(None, ("rows", "sub")), P())
    return jax.shard_map(local, mesh=mesh, in_specs=in_specs, out_specs=out_specs, check_vma=False)
```

profile of v0, /device:TPU:0, one launch (start us, length us, event | category | flops | bytes accessed | tf_op | source)
XLA Modules:
  0.0 229.9 jit_solution(9403381852364649270)
XLA Ops:
  0.7 10.1 %fusion.16 = f32[120,120]{0,1:T(8,128)S(1)} fusion(f32[120,16384]{1,0:T(8,128)} %param.5), kind=kOutput, calls=%fused_computation.44 | convolution fusion | flops 2831155200 | bytes 7921920 | tf_op jit(solution)/shard_map/kn,jn->kj/dot_general | solution.py:20
  10.8 6.2 %convolution_bitcast_fusion.3 = f32[120]{0:T(128)S(1)} fusion(f32[120,16384]{1,0:T(8,128)S(1)} %copy-done.1, f32[1,16384]{1,0:T(1,128)S(1)} %copy-done.2), kind=kOutput, calls=%fused_computation.10 | convolution fusion | flops 23592960 | bytes 7930336 | tf_op jit(solution)/shard_map/kn,n->k/dot_general | solution.py:21
  16.9 42.8 %all-reduce = (f32[120,120]{0,1:T(8,128)S(1)}, f32[120]{0:T(128)S(1)}) all-reduce(f32[120,120]{0,1:T(8,128)S(1)} %fusion.16, f32[120]{0:T(128)S(1)} %convolution_bitcast_fusion.3), channel_id=1, replica_groups=mesh['rows'=8,'sub'=4] {'rows','sub'}, use_global_device_ids=true, to_apply=%region_1.2 | all-reduce | flops 14520 | bytes 116160 | tf_op jit(solution)/shard_map/psum | solution.py:22
  59.9 11.0 %cholesky.16 = f32[120,120]{1,0:T(8,128)S(1)} custom-call(f32[120,120]{1,0:T(8,128)S(1)} %fusion.9), custom_call_target="Cholesky" | custom-call | tf_op jit(solution)/shard_map/jit(cholesky)/cholesky | solution.py:23
  70.9 0.6 compare_reduce_fusion
  71.5 0.7 select_bitcast_fusion
  72.2 9.2 %custom-call.10 = f32[1,120,120]{1,2,0:T(8,128)S(1)} custom-call(f32[1,120,120]{2,1,0:T(8,128)S(1)} %select_bitcast_fusion), custom_call_target="InvertDiagBlocksLowerTriangular" | custom-call | tf_op jit(solution)/shard_map/triangular_solve | solution.py:24
  81.8 6.7 %multiply_reduce_fusion = (f32[]{:T(128)}, f32[1,16384]{1,0:T(1,128)S(1)}) fusion(f32[1,16384]{1,0:T(1,128)S(1)} %copy-done.2, f32[120,1]{0,1:T(1,128)S(1)} %fusion.1, f32[120,16384]{1,0:T(8,128)} %param.5), kind=kOutput, calls=%fused_computation.15 | convolution fusion | flops 23642112 | bytes 7995876 | tf_op jit(solution)/shard_map/k,kn->n/dot_general | solution.py:38
  88.5 40.3 %psum.23 = f32[]{:T(128)} all-reduce(f32[]{:T(128)} %get-tuple-element.7), channel_id=1, replica_groups=mesh['rows'=8,'sub'=4] {'rows','sub'}, use_global_device_ids=true, to_apply=%region_6.7 | all-reduce | flops 1 | bytes 8 | tf_op jit(solution)/shard_map/psum | solution.py:39
  129.5 0.7 broadcast_multiply_fusion
  130.1 5.4 %all-to-all-start.1 = ((f32[1,32,512]{2,0,1:T(1,128)}), f32[1,32,512]{2,0,1:T(1,128)S(1)}, u32[]{:S(2)}, u32[]{:S(2)}) async-start(f32[1,32,512]{2,0,1:T(1,128)} %bitcast.14), calls=%async_computation.1 | async-start | bytes 131072 | tf_op jit(solution)/shard_map/all_to_all | solution.py:43
  135.8 6.5 %fusion.17 = f32[40,16384]{1,0:T(8,128)S(1)} fusion(f32[120,40]{0,1:T(8,128)S(1)} %fusion.7, f32[120,16384]{1,0:T(8,128)} %param.5), kind=kOutput, calls=%fused_computation.45 | convolution fusion | flops 943718400 | bytes 10504960 | tf_op jit(solution)/shard_map/kp,kn->pn/dot_general | solution.py:27
  142.3 1.7 copy.36
  144.1 1.7 sort.17
  145.8 5.8 %all-to-all-start = ((f32[40,32,512]{2,0,1:T(8,128)}), f32[40,32,512]{2,0,1:T(8,128)S(1)}, u32[]{:S(2)}, u32[]{:S(2)}) async-start(f32[40,32,512]{2,0,1:T(8,128)} %bitcast.69), calls=%async_computation | async-start | bytes 5242880 | tf_op jit(solution)/shard_map/all_to_all | solution.py:42
  151.8 67.3 %all_gather.3 = f32[3,120,120]{1,0,2:T(4,128)S(1)} all-gather(f32[3,120,30]{1,0,2:T(4,128)S(1)} %copy.21), channel_id=1, replica_groups=mesh['rows'=8,'sub'=4] {'sub'}, dimensions={2}, use_global_device_ids=true | all-gather | bytes 216000 | tf_op jit(solution)/shard_map/all_gather | solution.py:48
  219.1 0.9 convolution_bitcast_fusion
  220.0 1.0 multiply_reduce_fusion.1
  221.9 0.6 multiply_bitcast_fusion
  222.5 0.6 gather_fusion.1
  223.2 0.7 broadcast_select_fusion.1
  223.9 2.2 gather_fusion
  226.2 2.1 copy.26
  228.2 1.7 broadcast_select_fusion
  (30 shorter events, 1.1 us)
Async XLA Ops:
  0.6 134.9 %copy-start = (f32[120,40]{0,1:T(8,128)S(1)}, f32[120,40]{0,1:T(8,128)}, u32[]{:S(2)}) copy-start(f32[120,40]{0,1:T(8,128)} %param.8) | copy-start | bytes 57604
  0.6 10.1 %copy-start.1 = (f32[120,16384]{1,0:T(8,128)S(1)}, f32[120,16384]{1,0:T(8,128)}, u32[]{:S(2)}) copy-start(f32[120,16384]{1,0:T(8,128)} %param.5) | copy-start | bytes 23592964
  0.7 10.1 %copy-start.2 = (f32[1,16384]{1,0:T(1,128)S(1)}, f32[1,16384]{1,0:T(1,128)}, u32[]{:S(2)}) copy-start(f32[1,16384]{1,0:T(1,128)} %param.6) | copy-start | bytes 196612
  130.1 15.6 %all-to-all-start.1 = ((f32[1,32,512]{2,0,1:T(1,128)}), f32[1,32,512]{2,0,1:T(1,128)S(1)}, u32[]{:S(2)}, u32[]{:S(2)}) async-start(f32[1,32,512]{2,0,1:T(1,128)} %bitcast.14), calls=%async_computation.1 | async-start | bytes 131072 | tf_op jit(solution)/shard_map/all_to_all | solution.py:43
  135.8 8.3 %copy-start.4 = (s32[1,32]{1,0:T(1,128)S(1)}, s32[1,32]{1,0:T(1,128)}, u32[]{:S(2)}) copy-start(s32[1,32]{1,0:T(1,128)} %param.7) | copy-start | bytes 388
  142.3 9.4 %copy-start.3 = (f32[3,120,30]{1,2,0:T(8,128)S(1)}, f32[3,120,30]{1,2,0:T(8,128)}, u32[]{:S(2)}) copy-start(f32[3,120,30]{1,2,0:T(8,128)} %param.9) | copy-start | bytes 129604
  145.8 78.2 %all-to-all-start = ((f32[40,32,512]{2,0,1:T(8,128)}), f32[40,32,512]{2,0,1:T(8,128)S(1)}, u32[]{:S(2)}, u32[]{:S(2)}) async-start(f32[40,32,512]{2,0,1:T(8,128)} %bitcast.69), calls=%async_computation | async-start | bytes 5242880 | tf_op jit(solution)/shard_map/all_to_all | solution.py:42
where the time goes:
time: 231 us; the launch traced here: 230 us
  blocking collectives  150 us (65%)
  matrix products  32 us (14%)
  other arithmetic  27 us (12%)
  starting transfers between devices  11.2 us (5%)
  local copies, waits for them, and re-layouts  7.06 us (3%)
    all_gather x1, blocking collectives, local(): coeff_all = lax.all_gather(coeff, 'sub', axis=2, tiled=True)  67.3 us
    psum x1, blocking collectives, local(): gram_sum = lax.psum(gram_local, ('rows', 'sub'))  42.8 us
    psum x1, blocking collectives, local(): norm_sum = lax.psum(jnp.sum(remainder * remainder), ('rows', 'sub'))  40.3 us
    another operation x3, other arithmetic, local(): chol_lower = jnp.linalg.cholesky(gram_sum / nrows_all)  11.6 us
    dot_general x1, matrix products, local(): jnp.einsum('kn,jn->kj', basis_rows, basis_rows, precision=highest)  10.1 us
    another operation x2, other arithmetic, local(): lax.linalg.triangular_solve(chol_lower, restart, left_side=True, lower=Tr...  9.85 us
    dot_general x1, matrix products, local(): jnp.einsum('k,kn->n', proj_coef, basis_rows, precision=highest)[None, :]  6.74 us
    dot_general x1, matrix products, local(): new_rows = jnp.einsum('kp,kn->pn', factor, basis_rows, precision=highest)  6.51 us
  transfers between devices with their start and end apart: 2, of which 0 were waited for; matrix products, arithmetic and copies ran while one was open for 6% of the time, Pallas kernels for 0%

commit v1 on v0

--- a/solution.py
+++ b/solution.py
@@ -19,7 +19,7 @@
     basis_rows, resid_row = (u_fem, resid_fem)
     gram_local = jnp.einsum("kn,jn->kj", basis_rows, basis_rows, precision=highest)
     inner_local = jnp.einsum("kn,n->k", basis_rows, resid_row[0], precision=highest)
-    gram_sum = lax.psum(gram_local, ("rows", "sub"))
+    gram_sum = lax.psum(lax.psum(gram_local, "rows"), "sub")
     chol_lower = jnp.linalg.cholesky(gram_sum / nrows_all)
     factor = lax.linalg.triangular_solve(
         chol_lower, restart, left_side=True, lower=True, transpose_a=True

time: 231 us -> 273 us (1.18)
  blocking collectives: 150 us -> 192 us
    psum x1 -> x3, blocking collectives: 42.8 us -> 83.5 us  [the longest x2 46 us: local(): gram_sum = lax.psum(lax.psum(gram_local, 'rows'), 'sub')]
  transfers between devices with their start and end apart: 2 -> 2, of which waited for: 0 -> 0; matrix products, arithmetic and copies ran while one was open for 6% -> 5% of each run, Pallas kernels for 0% -> 0%
where the time goes in v1:
time: 273 us
  blocking collectives  192 us (70%)
  matrix products  34.1 us (12%)
  other arithmetic  27 us (10%)
  starting transfers between devices  10.6 us (4%)
  local copies, waits for them, and re-layouts  6.97 us (3%)
    all_gather x1, blocking collectives, local(): coeff_all = lax.all_gather(coeff, 'sub', axis=2, tiled=True)  67.3 us
    psum x2, blocking collectives, local(): gram_sum = lax.psum(lax.psum(gram_local, 'rows'), 'sub')  46 us
    psum x1, blocking collectives, local(): norm_sum = lax.psum(jnp.sum(remainder * remainder), ('rows', 'sub'))  40.9 us
    psum x1, blocking collectives, local(): inner_prod = lax.psum(inner_local, ('rows', 'sub'))  37.4 us
    another operation x3, other arithmetic, local(): chol_lower = jnp.linalg.cholesky(gram_sum / nrows_all)  11.6 us
    dot_general x1, matrix products, local(): jnp.einsum('kn,jn->kj', basis_rows, basis_rows, precision=highest)  9.95 us
    another operation x2, other arithmetic, local(): lax.linalg.triangular_solve(chol_lower, restart, left_side=True, lower=Tr...  9.85 us
    dot_general x1, matrix products, local(): jnp.einsum('kn,n->k', basis_rows, resid_row[0], precision=highest)  8.42 us
  transfers between devices with their start and end apart: 2, of which 0 were waited for; matrix products, arithmetic and copies ran while one was open for 5% of the time, Pallas kernels for 0%

profile of v1, /device:TPU:0, one launch (start us, length us, event | category | flops | bytes accessed | tf_op | source)
XLA Modules:
  0.0 272.5 jit_solution(14905371368036276439)
XLA Ops:
  0.7 9.9 %fusion.16 = f32[120,120]{0,1:T(8,128)S(1)} fusion(f32[120,16384]{1,0:T(8,128)} %param.5), kind=kOutput, calls=%fused_computation.44 | convolution fusion | flops 2831155200 | bytes 7921920 | tf_op jit(solution)/shard_map/kn,jn->kj/dot_general | solution.py:20
  10.6 26.1 %psum.28 = f32[120,120]{0,1:T(8,128)S(1)} all-reduce(f32[120,120]{0,1:T(8,128)S(1)} %fusion.16), channel_id=1, replica_groups=mesh['rows'=8,'sub'=4] {'rows'}, use_global_device_ids=true, to_apply=%region_1.2 | all-reduce | flops 14400 | bytes 115200 | tf_op jit(solution)/shard_map/psum | solution.py:22
  36.7 19.9 %psum.29 = f32[120,120]{0,1:T(8,128)S(1)} all-reduce(f32[120,120]{0,1:T(8,128)S(1)} %psum.28), channel_id=1, replica_groups=mesh['rows'=8,'sub'=4] {'sub'}, use_global_device_ids=true, to_apply=%region_2.3 | all-reduce | flops 14400 | bytes 115200 | tf_op jit(solution)/shard_map/psum | solution.py:22
  56.8 11.0 %cholesky.16 = f32[120,120]{1,0:T(8,128)S(1)} custom-call(f32[120,120]{1,0:T(8,128)S(1)} %fusion.9), custom_call_target="Cholesky" | custom-call | tf_op jit(solution)/shard_map/jit(cholesky)/cholesky | solution.py:23
  67.8 0.6 compare_reduce_fusion
  68.4 0.7 select_bitcast_fusion
  69.1 9.2 %custom-call.10 = f32[1,120,120]{1,2,0:T(8,128)S(1)} custom-call(f32[1,120,120]{2,1,0:T(8,128)S(1)} %select_bitcast_fusion), custom_call_target="InvertDiagBlocksLowerTriangular" | custom-call | tf_op jit(solution)/shard_map/triangular_solve | solution.py:24
  78.3 8.4 %convolution_bitcast_fusion.3 = f32[120]{0:T(128)S(1)} fusion(f32[120,16384]{1,0:T(8,128)} %param.5, f32[1,16384]{1,0:T(1,128)S(1)} %copy-done.1), kind=kOutput, calls=%fused_computation.10 | convolution fusion | flops 23592960 | bytes 7930336 | tf_op jit(solution)/shard_map/kn,n->k/dot_general | solution.py:21
  86.7 37.4 %psum.30 = f32[120]{0:T(128)S(1)} all-reduce(f32[120]{0:T(128)S(1)} %convolution_bitcast_fusion.3), channel_id=1, replica_groups=mesh['rows'=8,'sub'=4] {'rows','sub'}, use_global_device_ids=true, to_apply=%region_5.6 | all-reduce | flops 120 | bytes 960 | tf_op jit(solution)/shard_map/psum | solution.py:28
  124.5 6.7 %multiply_reduce_fusion = (f32[]{:T(128)}, f32[1,16384]{1,0:T(1,128)S(1)}) fusion(f32[1,16384]{1,0:T(1,128)S(1)} %copy-done.1, f32[120,1]{0,1:T(1,128)S(1)} %fusion.1, f32[120,16384]{1,0:T(8,128)} %param.5), kind=kOutput, calls=%fused_computation.15 | convolution fusion | flops 23642112 | bytes 7995876 | tf_op jit(solution)/shard_map/k,kn->n/dot_general | solution.py:38
  131.3 40.9 %psum.31 = f32[]{:T(128)} all-reduce(f32[]{:T(128)} %get-tuple-element.5), channel_id=1, replica_groups=mesh['rows'=8,'sub'=4] {'rows','sub'}, use_global_device_ids=true, to_apply=%region_7.8 | all-reduce | flops 1 | bytes 8 | tf_op jit(solution)/shard_map/psum | solution.py:39
  172.8 0.7 broadcast_multiply_fusion
  173.5 4.8 %all-to-all-start.1 = ((f32[1,32,512]{2,0,1:T(1,128)}), f32[1,32,512]{2,0,1:T(1,128)S(1)}, u32[]{:S(2)}, u32[]{:S(2)}) async-start(f32[1,32,512]{2,0,1:T(1,128)} %bitcast.14), calls=%async_computation.1 | async-start | bytes 131072 | tf_op jit(solution)/shard_map/all_to_all | solution.py:43
  178.5 6.5 %fusion.17 = f32[40,16384]{1,0:T(8,128)S(1)} fusion(f32[120,40]{0,1:T(8,128)S(1)} %fusion.7, f32[120,16384]{1,0:T(8,128)} %param.5), kind=kOutput, calls=%fused_computation.45 | convolution fusion | flops 943718400 | bytes 10504960 | tf_op jit(solution)/shard_map/kp,kn->pn/dot_general | solution.py:27
  185.1 1.7 copy.36
  186.8 1.7 sort.17
  188.5 5.8 %all-to-all-start = ((f32[40,32,512]{2,0,1:T(8,128)}), f32[40,32,512]{2,0,1:T(8,128)S(1)}, u32[]{:S(2)}, u32[]{:S(2)}) async-start(f32[40,32,512]{2,0,1:T(8,128)} %bitcast.69), calls=%async_computation | async-start | bytes 5242880 | tf_op jit(solution)/shard_map/all_to_all | solution.py:42
  194.5 67.3 %all_gather.3 = f32[3,120,120]{1,0,2:T(4,128)S(1)} all-gather(f32[3,120,30]{1,0,2:T(4,128)S(1)} %copy.21), channel_id=1, replica_groups=mesh['rows'=8,'sub'=4] {'sub'}, dimensions={2}, use_global_device_ids=true | all-gather | bytes 216000 | tf_op jit(solution)/shard_map/all_gather | solution.py:48
  261.8 0.9 convolution_bitcast_fusion
  262.7 1.0 multiply_reduce_fusion.1
  265.9 0.7 broadcast_select_fusion.1
  266.7 2.2 gather_fusion
  268.9 2.0 copy.26
  270.8 1.7 broadcast_select_fusion
  (30 shorter events, 2.4 us)
Async XLA Ops:
  0.6 177.6 %copy-start = (f32[120,40]{0,1:T(8,128)S(1)}, f32[120,40]{0,1:T(8,128)}, u32[]{:S(2)}) copy-start(f32[120,40]{0,1:T(8,128)} %param.8) | copy-start | bytes 57604
  0.6 77.7 %copy-start.1 = (f32[1,16384]{1,0:T(1,128)S(1)}, f32[1,16384]{1,0:T(1,128)}, u32[]{:S(2)}) copy-start(f32[1,16384]{1,0:T(1,128)} %param.6) | copy-start | bytes 196612
  173.5 15.0 %all-to-all-start.1 = ((f32[1,32,512]{2,0,1:T(1,128)}), f32[1,32,512]{2,0,1:T(1,128)S(1)}, u32[]{:S(2)}, u32[]{:S(2)}) async-start(f32[1,32,512]{2,0,1:T(1,128)} %bitcast.14), calls=%async_computation.1 | async-start | bytes 131072 | tf_op jit(solution)/shard_map/all_to_all | solution.py:43
  178.5 8.3 %copy-start.3 = (s32[1,32]{1,0:T(1,128)S(1)}, s32[1,32]{1,0:T(1,128)}, u32[]{:S(2)}) copy-start(s32[1,32]{1,0:T(1,128)} %param.7) | copy-start | bytes 388
  185.0 9.4 %copy-start.2 = (f32[3,120,30]{1,2,0:T(8,128)S(1)}, f32[3,120,30]{1,2,0:T(8,128)}, u32[]{:S(2)}) copy-start(f32[3,120,30]{1,2,0:T(8,128)} %param.9) | copy-start | bytes 129604
  188.5 78.2 %all-to-all-start = ((f32[40,32,512]{2,0,1:T(8,128)}), f32[40,32,512]{2,0,1:T(8,128)S(1)}, u32[]{:S(2)}, u32[]{:S(2)}) async-start(f32[40,32,512]{2,0,1:T(8,128)} %bitcast.69), calls=%async_computation | async-start | bytes 5242880 | tf_op jit(solution)/shard_map/all_to_all | solution.py:42
